TPU v7x, 512 devices: a whole 4x8x8 slice. The times are simulated.
512 devices in a mesh: dp: 32 (over z, y_hi), tensor: 16 (over x, y_lo, core).
Axes of the slice: x: 4, y: 8 (y_hi: 4, y_lo: 2; y = y_hi * 2 + y_lo), z: 8, core: 2. Of those that a mesh axis runs over, the one named last changes fastest.
Arguments:
- tokens_in: bfloat16 [4096, 4096], P(('dp', 'tensor')), may hold values from -6 to 6
- grad_out: bfloat16 [4096, 4096], P(('dp', 'tensor')), may hold values from -6 to 6
- gate_pre: bfloat16 [4096, 7168], P('dp', 'tensor'), may hold values from -6 to 6
- up_pre: bfloat16 [4096, 7168], P('dp', 'tensor'), may hold values from -6 to 6
- gate_weight: bfloat16 [4096, 7168], P('dp', 'tensor'), may hold values from -0.09375 to 0.09375
- up_weight: bfloat16 [4096, 7168], P('dp', 'tensor'), may hold values from -0.09375 to 0.09375
- down_weight: bfloat16 [7168, 4096], P('tensor', 'dp'), may hold values from -0.0625 to 0.0625
- norm_gain: float32 [4096], replicated, may hold values from 0.1 to 1.9
Outputs:
- input_grad: bfloat16 [4096, 4096], P(('dp', 'tensor'))
- gain_grad: float32 [4096], replicated
- down_grad: bfloat16 [7168, 4096], P('tensor', 'dp')
All inputs are finite; a program needn't handle non-finite values.
Results may differ from a plain program's by a relative error of at most 0.015.
Values may be sent and summed in bfloat16 or wider, within the bound.
A program may use at most 64 MiB of HBM per device.

v0:
```python
import jax
import jax.numpy as jnp
from jax import lax
from jax.sharding import Mesh
from jax.sharding import PartitionSpec as P

Z = "dp_0"
YH = "dp_1"
TENSOR = ("tensor_0", "tensor_1", "tensor_2")
DP = ("dp_0", "dp_1")
DP_TENSOR = ("dp_0", "dp_1", "tensor_0", "tensor_1", "tensor_2")


def nt(a, b):
    return lax.dot_general(a, b, (((1,), (1,)), ((), ())), preferred_element_type=jnp.float32)


def tn(a, b):
    return lax.dot_general(a, b, (((0,), (0,)), ((), ())), preferred_element_type=jnp.float32)


def swap(x, axis):
    return lax.all_to_all(x, axis, split_axis=0, concat_axis=0, tiled=True)


def per_device(
    tokens_in, grad_out, gate_pre, up_pre, gate_weight, up_weight, down_weight, norm_gain
):
    mine = swap(grad_out.reshape(8, 8, 4, 128).transpose(2, 0, 1, 3), YH)
    rows = lax.all_gather(mine.reshape(32, 1024), TENSOR, axis=0, tiled=True)
    rows = rows.reshape(16, 4, 8, 1024).transpose(1, 0, 2, 3).reshape(512, 1024)
    down = lax.all_gather(down_weight, Z, axis=1, tiled=True)
    gate_w = lax.all_gather(gate_weight, Z, axis=0, tiled=True)
    up_w = lax.all_gather(up_weight, Z, axis=0, tiled=True)
    gate = lax.all_gather(gate_pre, YH, axis=0, tiled=True).astype(jnp.float32)
    up = lax.all_gather(up_pre, YH, axis=0, tiled=True).astype(jnp.float32)
    sig = jax.nn.sigmoid(gate)
    silu = gate * sig
    act = (silu * up).astype(jnp.bfloat16)
    part = nt(rows, down).astype(jnp.bfloat16).reshape(4, 128, 448)
    grad_act = swap(part, YH).astype(jnp.float32).sum(axis=0).astype(jnp.bfloat16)
    grad_act = lax.all_gather(grad_act, YH, axis=0, tiled=True).astype(jnp.float32)
    grad_gate = (grad_act * up * sig * (1.0 + gate * (1.0 - sig))).astype(jnp.bfloat16)
    grad_up = (grad_act * silu).astype(jnp.bfloat16)
    norm = (nt(grad_gate, gate_w) + nt(grad_up, up_w)).astype(jnp.bfloat16)
    norm = norm.reshape(4, 16, 8, 1024).transpose(1, 0, 2, 3)
    norm = swap(norm, TENSOR).astype(jnp.float32).sum(axis=0)
    norm = swap(norm, YH).reshape(4, 8, 8, 128)
    grad_norm = norm.transpose(1, 2, 0, 3).reshape(8, 4096)
    total = tn(act, rows).astype(jnp.bfloat16).reshape(448, 8, 128).transpose(1, 0, 2)
    down_grad = swap(total, Z).astype(jnp.float32).sum(axis=0).astype(jnp.bfloat16)
    inputs = tokens_in.astype(jnp.float32)
    inv_rms = lax.rsqrt(jnp.mean(inputs * inputs, axis=1, keepdims=True) + 1e-05)
    normed = inputs * inv_rms
    gain_grad = lax.psum(jnp.sum(grad_norm * normed, axis=0), DP_TENSOR)
    scaled = grad_norm * norm_gain
    inner = jnp.mean(scaled * normed, axis=1, keepdims=True)
    input_grad = (grad_out.astype(jnp.float32) + inv_rms * (scaled - normed * inner)).astype(
        jnp.bfloat16
    )
    return (input_grad, gain_grad, down_grad)


def solution(mesh):
    finer = Mesh(
        mesh.devices.reshape(8, 4, 4, 2, 2), ("dp_0", "dp_1", "tensor_0", "tensor_1", "tensor_2")
    )
    return jax.shard_map(
        per_device,
        mesh=finer,
        in_specs=(
            P(DP_TENSOR, None),
            P(DP_TENSOR, None),
            P(DP, TENSOR),
            P(DP, TENSOR),
            P(DP, TENSOR),
            P(DP, TENSOR),
            P(TENSOR, DP),
            P(),
        ),
        out_specs=(P(DP_TENSOR, None), P(), P(TENSOR, DP)),
        check_vma=False,
    )
```

profile of v0, /device:TPU:1, one launch (start us, length us, event | category | flops | bytes accessed | tf_op | source)
XLA Modules:
  0.0 346.4 jit_solution(479711068150174751)
XLA Ops:
  7.2 0.0 all-gather.2.cloned.1.call-start
  7.2 0.9 copy.37
  8.1 14.3 %all_to_all.25 = bf16[4,8,8,128]{3,2,1,0:T(8,128)(2,1)S(1)} all-to-all(bf16[4,8,8,128]{3,2,1,0:T(8,128)(2,1)S(1)} %bitcast.51), channel_id=1, replica_groups=mesh['dp_0'=8,'dp_1'=4,'tensor_0'=4,'tensor_1'=2,'tensor_2'=2] {'dp_1'}, dimensions={0} | all-to-all | bytes 131072 | tf_op jit(solution)/shard_map/all_to_all | solution.py:23
  22.4 0.6 copy.36
  23.0 0.0 all-gather.2.cloned.1.call-update
  23.1 28.1 %all_gather.26 = bf16[1024,448]{0,1:T(8,128)(2,1)S(1)} all-gather(bf16[128,448]{0,1:T(8,128)(2,1)} %param.12), channel_id=1, replica_groups=mesh['dp_0'=8,'dp_1'=4,'tensor_0'=4,'tensor_1'=2,'tensor_2'=2] {'dp_0'}, dimensions={0}, use_global_device_ids=true | all-gather | bytes 1032192 | tf_op jit(solution)/shard_map/all_gather | solution.py:33
  51.2 22.6 %all_gather.22 = bf16[448,1024]{1,0:T(8,128)(2,1)S(1)} all-gather(bf16[448,128]{1,0:T(8,128)(2,1)} %param.14), channel_id=1, replica_groups=mesh['dp_0'=8,'dp_1'=4,'tensor_0'=4,'tensor_1'=2,'tensor_2'=2] {'dp_0'}, dimensions={1}, use_global_device_ids=true | all-gather | bytes 1032192 | tf_op jit(solution)/shard_map/all_gather | solution.py:32
  73.7 1.3 copy.17
  75.1 0.0 copy-start.5
  75.1 0.7 fusion.1
  75.7 0.0 copy-start.6
  75.8 0.8 copy.34
  76.6 3.5 all-to-all-start.1
  80.1 0.0 copy-done.5
  80.1 23.9 %all_gather.25 = bf16[512,448]{0,1:T(8,128)(2,1)S(1)} all-gather(bf16[128,448]{0,1:T(8,128)(2,1)S(1)} %copy-done.5), channel_id=1, replica_groups=mesh['dp_0'=8,'dp_1'=4,'tensor_0'=4,'tensor_1'=2,'tensor_2'=2] {'dp_1'}, dimensions={0}, use_global_device_ids=true | all-gather | bytes 573440 | tf_op jit(solution)/shard_map/all_gather | solution.py:35
  104.0 0.0 copy-done.6
  104.0 16.0 %all_gather.24 = bf16[512,448]{0,1:T(8,128)(2,1)S(1)} all-gather(bf16[128,448]{0,1:T(8,128)(2,1)S(1)} %copy-done.6), channel_id=1, replica_groups=mesh['dp_0'=8,'dp_1'=4,'tensor_0'=4,'tensor_1'=2,'tensor_2'=2] {'dp_1'}, dimensions={0}, use_global_device_ids=true | all-gather | bytes 573440 | tf_op jit(solution)/shard_map/all_gather | solution.py:36
  120.0 20.3 %all_gather.27 = bf16[1024,448]{0,1:T(8,128)(2,1)} all-gather(bf16[128,448]{0,1:T(8,128)(2,1)} %param.13), channel_id=1, replica_groups=mesh['dp_0'=8,'dp_1'=4,'tensor_0'=4,'tensor_1'=2,'tensor_2'=2] {'dp_0'}, dimensions={0}, use_global_device_ids=true | all-gather | bytes 1032192 | tf_op jit(solution)/shard_map/all_gather | solution.py:34
  140.4 0.0 all-to-all-done.1
  140.4 0.1 reduce_sum.61
  140.4 16.1 %all_gather.23 = bf16[512,448]{0,1:T(8,128)(2,1)S(1)} all-gather(bf16[128,448]{0,1:T(8,128)(2,1)S(1)} %reduce_sum.61), channel_id=1, replica_groups=mesh['dp_0'=8,'dp_1'=4,'tensor_0'=4,'tensor_1'=2,'tensor_2'=2] {'dp_1'}, dimensions={0}, use_global_device_ids=true | all-gather | bytes 573440 | tf_op jit(solution)/shard_map/all_gather | solution.py:42
  156.6 0.9 fusion.11
  157.5 0.0 copy-done.2
  157.5 0.2 copy-done
  157.8 0.8 add_convert_fusion
  158.6 1.1 copy.32
  159.7 25.8 %all-to-all-start.2 = ((bf16[16,4,8,1024]{3,2,1,0:T(8,128)(2,1)}), bf16[16,4,8,1024]{3,2,1,0:T(8,128)(2,1)S(1)}, u32[]{:S(2)}, u32[]{:S(2)}) async-start(bf16[16,4,8,1024]{3,2,1,0:T(8,128)(2,1)} %bitcast.36), calls=%async_computation.2 | async-start | bytes 2097152 | tf_op jit(solution)/shard_map/all_to_all | solution.py:23
  185.5 0.0 copy-done.3
  185.5 0.7 fusion
  186.2 0.0 copy-start.1
  186.2 1.1 copy.33
  187.4 13.8 %all-to-all-done.2 = bf16[16,4,8,1024]{3,2,1,0:T(8,128)(2,1)S(1)} async-done(((bf16[16,4,8,1024]{3,2,1,0:T(8,128)(2,1)}), bf16[16,4,8,1024]{3,2,1,0:T(8,128)(2,1)S(1)}, u32[]{:S(2)}, u32[]{:S(2)}) %all-to-all-start.2) | async-done | bytes 1048608 | tf_op jit(solution)/shard_map/all_to_all | solution.py:23
  201.1 4.5 %all-to-all-start.4 = ((bf16[8,448,128]{2,1,0:T(8,128)(2,1)}), bf16[8,448,128]{2,1,0:T(8,128)(2,1)S(1)}, u32[]{:S(2)}, u32[]{:S(2)}) async-start(bf16[8,448,128]{2,1,0:T(8,128)(2,1)} %bitcast.38), calls=%async_computation.4 | async-start | bytes 1835008 | tf_op jit(solution)/shard_map/all_to_all | solution.py:23
  205.6 0.0 copy-start.7
  205.6 0.0 copy-start.4
  205.6 0.1 fusion.25
  205.8 0.8 convert_reduce_fusion
  206.6 25.4 %all-to-all-done.4 = bf16[8,448,128]{2,1,0:T(8,128)(2,1)S(1)} async-done(((bf16[8,448,128]{2,1,0:T(8,128)(2,1)}), bf16[8,448,128]{2,1,0:T(8,128)(2,1)S(1)}, u32[]{:S(2)}, u32[]{:S(2)}) %all-to-all-start.4) | async-done | bytes 917536 | tf_op jit(solution)/shard_map/all_to_all | solution.py:23
  232.0 4.0 %all-to-all-start.3 = ((f32[4,8,1024]{2,1,0:T(8,128)}), f32[4,8,1024]{2,1,0:T(8,128)S(1)}, u32[]{:S(2)}, u32[]{:S(2)}) async-start(f32[4,8,1024]{2,1,0:T(8,128)} %convert_reduce_fusion), calls=%async_computation.3 | async-start | bytes 262144 | tf_op jit(solution)/shard_map/all_to_all | solution.py:23
  236.0 0.8 reduce_sum.65
  236.8 6.6 %all-to-all-done.3 = f32[4,8,1024]{2,1,0:T(8,128)S(1)} async-done(((f32[4,8,1024]{2,1,0:T(8,128)}), f32[4,8,1024]{2,1,0:T(8,128)S(1)}, u32[]{:S(2)}, u32[]{:S(2)}) %all-to-all-start.3) | async-done | bytes 131104 | tf_op jit(solution)/shard_map/all_to_all | solution.py:23
  243.4 0.1 copy.20
  243.5 0.1 reshape.53
  243.5 0.0 copy-done.7
  243.6 0.2 fusion.24
  243.8 95.1 %psum.7 = f32[4096]{0:T(1024)} all-reduce(f32[4096]{0:T(1024)S(1)} %get-tuple-element.3), channel_id=1, replica_groups=mesh['dp_0'=8,'dp_1'=4,'tensor_0'=4,'tensor_1'=2,'tensor_2'=2] {'dp_0','..., use_global_device_ids=true, to_apply=%region_5.0 | all-reduce | flops 4096 | bytes 32768 | tf_op jit(solution)/shard_map/psum | solution.py:55
  338.9 0.0 copy-done.4
  338.9 0.7 fusion.23
  (8 shorter events, 0.0 us)
Async XLA Ops:
  7.2 66.6 %all-gather.2.cloned.1.call-start = ((), (), s32[]{:S(2)}) async-start(), calls=%async_computation.5 | async-start | bytes 1114112 | tf_op jit(solution)/shard_map/all_gather | solution.py:30
  75.1 5.0 %copy-start.5 = (bf16[128,448]{0,1:T(8,128)(2,1)S(1)}, bf16[128,448]{0,1:T(8,128)(2,1)}, u32[]{:S(2)}) copy-start(bf16[128,448]{0,1:T(8,128)(2,1)} %param.10) | copy-start | bytes 344068
  75.7 28.2 %copy-start.6 = (bf16[128,448]{0,1:T(8,128)(2,1)S(1)}, bf16[128,448]{0,1:T(8,128)(2,1)}, u32[]{:S(2)}) copy-start(bf16[128,448]{0,1:T(8,128)(2,1)} %param.11) | copy-start | bytes 344068
  76.6 63.8 %all-to-all-start.1 = ((bf16[4,128,448]{1,2,0:T(8,128)(2,1)}), bf16[4,128,448]{1,2,0:T(8,128)(2,1)S(1)}, u32[]{:S(2)}, u32[]{:S(2)}) async-start(bf16[4,128,448]{1,2,0:T(8,128)(2,1)} %bitcast.39), calls=%async_computation.1 | async-start | bytes 917504 | tf_op jit(solution)/shard_map/all_to_all | solution.py:23
  120.0 37.5 %copy-start.2 = (bf16[512,448]{0,1:T(8,128)(2,1)}, bf16[512,448]{0,1:T(8,128)(2,1)S(1)}, u32[]{:S(2)}) copy-start(bf16[512,448]{0,1:T(8,128)(2,1)S(1)} %all_gather.24) | copy-start | bytes 1376260
  156.6 1.2 copy-start
  158.6 26.9 %copy-start.3 = (bf16[512,448]{0,1:T(8,128)(2,1)S(1)}, bf16[512,448]{0,1:T(8,128)(2,1)}, u32[]{:S(2)}) copy-start(bf16[512,448]{0,1:T(8,128)(2,1)} %copy-done.2) | copy-start | bytes 1376260
  159.7 41.5 %all-to-all-start.2 = ((bf16[16,4,8,1024]{3,2,1,0:T(8,128)(2,1)}), bf16[16,4,8,1024]{3,2,1,0:T(8,128)(2,1)S(1)}, u32[]{:S(2)}, u32[]{:S(2)}) async-start(bf16[16,4,8,1024]{3,2,1,0:T(8,128)(2,1)} %bitcast.36), calls=%async_computation.2 | async-start | bytes 2097152 | tf_op jit(solution)/shard_map/all_to_all | solution.py:23
  186.2 19.4 %copy-start.1 = (bf16[8,4096]{1,0:T(8,128)(2,1)S(1)}, bf16[8,4096]{1,0:T(8,128)(2,1)}, u32[]{:S(2)}) copy-start(bf16[8,4096]{1,0:T(8,128)(2,1)} %param.8) | copy-start | bytes 196612
  201.1 30.9 %all-to-all-start.4 = ((bf16[8,448,128]{2,1,0:T(8,128)(2,1)}), bf16[8,448,128]{2,1,0:T(8,128)(2,1)S(1)}, u32[]{:S(2)}, u32[]{:S(2)}) async-start(bf16[8,448,128]{2,1,0:T(8,128)(2,1)} %bitcast.38), calls=%async_computation.4 | async-start | bytes 1835008 | tf_op jit(solution)/shard_map/all_to_all | solution.py:23
  205.6 37.9 %copy-start.7 = (f32[4096]{0:T(1024)S(1)}, f32[4096]{0:T(1024)}, u32[]{:S(2)}) copy-start(f32[4096]{0:T(1024)} %param.15) | copy-start | bytes 49156
  205.6 133.2 %copy-start.4 = (bf16[8,4096]{1,0:T(8,128)(2,1)S(1)}, bf16[8,4096]{1,0:T(8,128)(2,1)}, u32[]{:S(2)}) copy-start(bf16[8,4096]{1,0:T(8,128)(2,1)} %param.9) | copy-start | bytes 196612
  232.0 11.4 %all-to-all-start.3 = ((f32[4,8,1024]{2,1,0:T(8,128)}), f32[4,8,1024]{2,1,0:T(8,128)S(1)}, u32[]{:S(2)}, u32[]{:S(2)}) async-start(f32[4,8,1024]{2,1,0:T(8,128)} %convert_reduce_fusion), calls=%async_computation.3 | async-start | bytes 262144 | tf_op jit(solution)/shard_map/all_to_all | solution.py:23
Sparse Core Ops, SparseCore 0:
  23.2 39.1 all-gather.1
where the time goes:
time: 347 us; the launch traced here: 346 us
  blocking collectives  236 us (68%)
  waiting for transfers between devices  45.7 us (13%)
  starting transfers between devices  37.8 us (11%)
  between operations  14.2 us (4%)
  local copies, waits for them, and re-layouts  6.3 us (2%)
    psum x1, blocking collectives, per_device(): gain_grad = lax.psum(jnp.sum(grad_norm * normed, axis=0), DP_TENSOR)  95.1 us
    all_to_all x4, waiting for transfers between devices, swap(): return lax.all_to_all(x, axis, split_axis=0, concat_axis=0, tiled=True)  45.7 us
    all_to_all x4, starting transfers between devices, swap(): return lax.all_to_all(x, axis, split_axis=0, concat_axis=0, tiled=True)  37.8 us
    all_gather x1, blocking collectives, per_device(): gate_w = lax.all_gather(gate_weight, Z, axis=0, tiled=True)  28.1 us
    all_gather x1, blocking collectives, per_device(): gate = lax.all_gather(gate_pre, YH, axis=0, tiled=True).astype(jnp.float32)  23.9 us
    all_gather x1, blocking collectives, per_device(): down = lax.all_gather(down_weight, Z, axis=1, tiled=True)  22.6 us
    all_gather x1, blocking collectives, per_device(): up_w = lax.all_gather(up_weight, Z, axis=0, tiled=True)  20.3 us
    all_gather x1, blocking collectives, per_device(): lax.all_gather(grad_act, YH, axis=0, tiled=True).astype(jnp.float32)  16.1 us
  transfers between devices with their start and end apart: 5, of which 3 were waited for; matrix products, arithmetic and copies ran while one was open for 1% of the time, Pallas kernels for 0%

commit v1 on v0

--- a/solution.py
+++ b/solution.py
@@ -31,7 +31,8 @@
     rows = rows.reshape(16, 4, 8, 1024).transpose(1, 0, 2, 3).reshape(512, 1024)
     down = lax.all_gather(down_weight, Z, axis=1, tiled=True)
     gate_w = lax.all_gather(gate_weight, Z, axis=0, tiled=True)
-    up_w = lax.all_gather(up_weight, Z, axis=0, tiled=True)
+    sent = jnp.stack([up_weight] * lax.axis_size(Z))
+    up_w = jnp.concatenate(lax.all_to_all(sent, Z, 0, 0), axis=0)
     gate = lax.all_gather(gate_pre, YH, axis=0, tiled=True).astype(jnp.float32)
     up = lax.all_gather(up_pre, YH, axis=0, tiled=True).astype(jnp.float32)
     sig = jax.nn.sigmoid(gate)

time: 347 us -> 351 us (1.012)
  waiting for transfers between devices: 45.7 us -> 57 us
  starting transfers between devices: 37.8 us -> 28.4 us
  matrix products: 3.15 us -> 7.42 us
    all_gather x1 -> x0, blocking collectives: 20.3 us -> none  [per_device(): up_w = lax.all_gather(up_weight, Z, axis=0, tiled=True)]
    all_to_all x1 -> x2, blocking collectives: 14.3 us -> 33.9 us  [swap(): return lax.all_to_all(x, axis, split_axis=0, concat_axis=0, tiled=True)]
    all_to_all x4 -> x3, starting transfers between devices: 37.8 us -> 21.9 us  [swap(): return lax.all_to_all(x, axis, split_axis=0, concat_axis=0, tiled=True)]
    all_gather x1, waiting for transfers between devices: 0.01 us -> 11.2 us  [per_device(): rows = lax.all_gather(mine.reshape(32, 1024), TENSOR, axis=0, tiled=True)]
    all_to_all x0 -> x1, starting transfers between devices: none -> 6.51 us  [per_device(): up_w = jnp.concatenate(lax.all_to_all(sent, Z, 0, 0), axis=0)]
    all_gather x1, blocking collectives: 22.6 us -> 28.1 us  [per_device(): down = lax.all_gather(down_weight, Z, axis=1, tiled=True)]
    all_gather x1, blocking collectives: 28.1 us -> 23 us  [per_device(): gate_w = lax.all_gather(gate_weight, Z, axis=0, tiled=True)]
    dot_general x3, matrix products: 2.43 us -> 6.69 us  [nt(): lax.dot_general(a, b, (((1,), (1,)), ((), ())), preferred_element_type=jn...]
  transfers between devices with their start and end apart: 5 -> 5, of which waited for: 3 -> 4; matrix products, arithmetic and copies ran while one was open for 1% -> 2% of each run, Pallas kernels for 0% -> 0%
where the time goes in v1:
time: 351 us; the launch traced here: 350 us
  blocking collectives  233 us (66%)
  waiting for transfers between devices  57 us (16%)
  starting transfers between devices  28.4 us (8%)
  between operations  14.2 us (4%)
  matrix products  7.42 us (2%)
  local copies, waits for them, and re-layouts  7.14 us (2%)
    psum x1, blocking collectives, per_device(): gain_grad = lax.psum(jnp.sum(grad_norm * normed, axis=0), DP_TENSOR)  95.1 us
    all_to_all x3, waiting for transfers between devices, swap(): return lax.all_to_all(x, axis, split_axis=0, concat_axis=0, tiled=True)  45.8 us
    all_to_all x2, blocking collectives, swap(): return lax.all_to_all(x, axis, split_axis=0, concat_axis=0, tiled=True)  33.9 us
    all_gather x1, blocking collectives, per_device(): down = lax.all_gather(down_weight, Z, axis=1, tiled=True)  28.1 us
    all_gather x1, blocking collectives, per_device(): gate_w = lax.all_gather(gate_weight, Z, axis=0, tiled=True)  23 us
    all_to_all x3, starting transfers between devices, swap(): return lax.all_to_all(x, axis, split_axis=0, concat_axis=0, tiled=True)  21.9 us
    all_gather x1, blocking collectives, per_device(): gate = lax.all_gather(gate_pre, YH, axis=0, tiled=True).astype(jnp.float32)  20.2 us
    all_gather x1, blocking collectives, per_device(): up = lax.all_gather(up_pre, YH, axis=0, tiled=True).astype(jnp.float32)  16.6 us
  transfers between devices with their start and end apart: 5, of which 4 were waited for; matrix products, arithmetic and copies ran while one was open for 2% of the time, Pallas kernels for 0%

profile of v1, /device:TPU:1, one launch (start us, length us, event | category | flops | bytes accessed | tf_op | source)
XLA Modules:
  0.0 350.1 jit_solution(10894852090322145741)
XLA Ops:
  7.2 0.0 all-gather.2.cloned.1.call-start
  7.2 0.9 copy.52
  8.1 14.3 %all_to_all.30 = bf16[4,8,8,128]{3,2,1,0:T(8,128)(2,1)S(1)} all-to-all(bf16[4,8,8,128]{3,2,1,0:T(8,128)(2,1)S(1)} %bitcast.58), channel_id=1, replica_groups=mesh['dp_0'=8,'dp_1'=4,'tensor_0'=4,'tensor_1'=2,'tensor_2'=2] {'dp_1'}, dimensions={0} | all-to-all | bytes 131072 | tf_op jit(solution)/shard_map/all_to_all | solution.py:23
  22.4 0.6 copy.51
  23.0 0.0 all-gather.2.cloned.1.call-update
  23.1 28.1 %all_gather.19 = bf16[448,1024]{1,0:T(8,128)(2,1)S(1)} all-gather(bf16[448,128]{1,0:T(8,128)(2,1)} %param.14), channel_id=1, replica_groups=mesh['dp_0'=8,'dp_1'=4,'tensor_0'=4,'tensor_1'=2,'tensor_2'=2] {'dp_0'}, dimensions={1}, use_global_device_ids=true | all-gather | bytes 1032192 | tf_op jit(solution)/shard_map/all_gather | solution.py:32
  51.2 11.2 %all-gather.2.cloned.1.call-done = bf16[512,1024]{1,0:T(8,128)(2,1)} async-done(((bf16[32,1024]{1,0:T(8,128)(2,1)}), bf16[512,1024]{1,0:T(8,128)(2,1)}) %all-gather.2.cloned.1.call-update) | async-done | bytes 1048592 | tf_op jit(solution)/shard_map/all_gather | solution.py:30
  62.4 1.3 copy.26
  63.7 0.0 copy-start.6
  63.7 0.7 fusion.1
  64.4 0.1 copy.49
  64.5 0.0 copy-start.7
  64.5 0.0 copy-start.8
  64.5 19.6 %all_to_all.31 = bf16[4,128,448]{1,2,0:T(8,128)(2,1)S(1)} all-to-all(bf16[4,128,448]{1,2,0:T(8,128)(2,1)S(1)} %bitcast.50), channel_id=1, replica_groups=mesh['dp_0'=8,'dp_1'=4,'tensor_0'=4,'tensor_1'=2,'tensor_2'=2] {'dp_1'}, dimensions={0} | all-to-all | bytes 917504 | tf_op jit(solution)/shard_map/all_to_all | solution.py:23
  84.1 0.0 copy-done.6
  84.1 1.0 stack.2
  85.1 6.5 %all-to-all-start.2 = ((bf16[8,128,448]{1,2,0:T(8,128)(2,1)}), bf16[8,128,448]{1,2,0:T(8,128)(2,1)S(1)}, u32[]{:S(2)}, u32[]{:S(2)}) async-start(bf16[8,128,448]{1,2,0:T(8,128)(2,1)} %stack.2), calls=%async_computation.2 | async-start | bytes 1835008 | tf_op jit(solution)/shard_map/all_to_all | solution.py:35
  91.7 20.2 %all_gather.22 = bf16[512,448]{0,1:T(8,128)(2,1)} all-gather(bf16[128,448]{0,1:T(8,128)(2,1)S(1)} %copy-done.7), channel_id=1, replica_groups=mesh['dp_0'=8,'dp_1'=4,'tensor_0'=4,'tensor_1'=2,'tensor_2'=2] {'dp_1'}, dimensions={0}, use_global_device_ids=true | all-gather | bytes 573440 | tf_op jit(solution)/shard_map/all_gather | solution.py:36
  111.9 0.0 copy-done.8
  111.9 16.6 %all_gather.21 = bf16[512,448]{0,1:T(8,128)(2,1)} all-gather(bf16[128,448]{0,1:T(8,128)(2,1)S(1)} %copy-done.8), channel_id=1, replica_groups=mesh['dp_0'=8,'dp_1'=4,'tensor_0'=4,'tensor_1'=2,'tensor_2'=2] {'dp_1'}, dimensions={0}, use_global_device_ids=true | all-gather | bytes 573440 | tf_op jit(solution)/shard_map/all_gather | solution.py:37
  128.5 23.0 %all_gather.23 = bf16[1024,448]{0,1:T(8,128)(2,1)S(1)} all-gather(bf16[128,448]{0,1:T(8,128)(2,1)S(1)} %copy-done.9), channel_id=1, replica_groups=mesh['dp_0'=8,'dp_1'=4,'tensor_0'=4,'tensor_1'=2,'tensor_2'=2] {'dp_0'}, dimensions={0}, use_global_device_ids=true | all-gather | bytes 1032192 | tf_op jit(solution)/shard_map/all_gather | solution.py:33
  151.5 0.1 reduce_sum.61
  151.6 16.2 %all_gather.20 = bf16[512,448]{0,1:T(8,128)(2,1)S(1)} all-gather(bf16[128,448]{0,1:T(8,128)(2,1)S(1)} %reduce_sum.61), channel_id=1, replica_groups=mesh['dp_0'=8,'dp_1'=4,'tensor_0'=4,'tensor_1'=2,'tensor_2'=2] {'dp_1'}, dimensions={0}, use_global_device_ids=true | all-gather | bytes 573440 | tf_op jit(solution)/shard_map/all_gather | solution.py:43
  167.8 0.8 copy-done.4
  168.6 3.5 fusion.13
  172.0 0.0 all-to-all-done.2
  172.0 2.5 add_convert_fusion
  174.6 1.1 copy.47
  175.7 14.0 %all-to-all-start.3 = ((bf16[16,4,8,1024]{3,2,1,0:T(8,128)(2,1)}), bf16[16,4,8,1024]{3,2,1,0:T(8,128)(2,1)S(1)}, u32[]{:S(2)}, u32[]{:S(2)}) async-start(bf16[16,4,8,1024]{3,2,1,0:T(8,128)(2,1)} %bitcast.42), calls=%async_computation.3 | async-start | bytes 2097152 | tf_op jit(solution)/shard_map/all_to_all | solution.py:23
  189.7 0.0 copy-done.2
  189.7 0.7 fusion
  190.5 0.0 copy-start
  190.5 1.2 copy.48
  191.6 13.8 %all-to-all-done.3 = bf16[16,4,8,1024]{3,2,1,0:T(8,128)(2,1)S(1)} async-done(((bf16[16,4,8,1024]{3,2,1,0:T(8,128)(2,1)}), bf16[16,4,8,1024]{3,2,1,0:T(8,128)(2,1)S(1)}, u32[]{:S(2)}, u32[]{:S(2)}) %all-to-all-start.3) | async-done | bytes 1048608 | tf_op jit(solution)/shard_map/all_to_all | solution.py:23
  205.5 4.2 %all-to-all-start.5 = ((bf16[8,448,128]{2,1,0:T(8,128)(2,1)}), bf16[8,448,128]{2,1,0:T(8,128)(2,1)S(1)}, u32[]{:S(2)}, u32[]{:S(2)}) async-start(bf16[8,448,128]{2,1,0:T(8,128)(2,1)} %bitcast.44), calls=%async_computation.5 | async-start | bytes 1835008 | tf_op jit(solution)/shard_map/all_to_all | solution.py:23
  209.6 0.0 copy-start.10
  209.6 0.0 copy-start.5
  209.7 0.1 fusion.27
  209.8 0.8 convert_reduce_fusion
  210.6 25.4 %all-to-all-done.5 = bf16[8,448,128]{2,1,0:T(8,128)(2,1)S(1)} async-done(((bf16[8,448,128]{2,1,0:T(8,128)(2,1)}), bf16[8,448,128]{2,1,0:T(8,128)(2,1)S(1)}, u32[]{:S(2)}, u32[]{:S(2)}) %all-to-all-start.5) | async-done | bytes 917536 | tf_op jit(solution)/shard_map/all_to_all | solution.py:23
  236.0 3.7 %all-to-all-start.4 = ((f32[4,8,1024]{2,1,0:T(8,128)}), f32[4,8,1024]{2,1,0:T(8,128)S(1)}, u32[]{:S(2)}, u32[]{:S(2)}) async-start(f32[4,8,1024]{2,1,0:T(8,128)} %convert_reduce_fusion), calls=%async_computation.4 | async-start | bytes 262144 | tf_op jit(solution)/shard_map/all_to_all | solution.py:23
  239.7 0.8 reduce_sum.65
  240.5 6.6 %all-to-all-done.4 = f32[4,8,1024]{2,1,0:T(8,128)S(1)} async-done(((f32[4,8,1024]{2,1,0:T(8,128)}), f32[4,8,1024]{2,1,0:T(8,128)S(1)}, u32[]{:S(2)}, u32[]{:S(2)}) %all-to-all-start.4) | async-done | bytes 131104 | tf_op jit(solution)/shard_map/all_to_all | solution.py:23
  247.0 0.1 copy.30
  247.1 0.1 reshape.59
  247.2 0.2 fusion.26
  247.4 95.1 %psum.7 = f32[4096]{0:T(1024)} all-reduce(f32[4096]{0:T(1024)S(1)} %get-tuple-element.3), channel_id=1, replica_groups=mesh['dp_0'=8,'dp_1'=4,'tensor_0'=4,'tensor_1'=2,'tensor_2'=2] {'dp_0','..., use_global_device_ids=true, to_apply=%region_5.0 | all-reduce | flops 4096 | bytes 32768 | tf_op jit(solution)/shard_map/psum | solution.py:56
  342.5 0.7 fusion.25
  (15 shorter events, 0.1 us)
Async XLA Ops:
  7.2 55.2 %all-gather.2.cloned.1.call-start = ((), (), s32[]{:S(2)}) async-start(), calls=%async_computation.6 | async-start | bytes 1114112 | tf_op jit(solution)/shard_map/all_gather | solution.py:30
  63.7 20.4 %copy-start.6 = (bf16[128,448]{0,1:T(8,128)(2,1)S(1)}, bf16[128,448]{0,1:T(8,128)(2,1)}, u32[]{:S(2)}) copy-start(bf16[128,448]{0,1:T(8,128)(2,1)} %param.13) | copy-start | bytes 344068
  64.5 27.2 %copy-start.7 = (bf16[128,448]{0,1:T(8,128)(2,1)S(1)}, bf16[128,448]{0,1:T(8,128)(2,1)}, u32[]{:S(2)}) copy-start(bf16[128,448]{0,1:T(8,128)(2,1)} %param.10) | copy-start | bytes 344068
  64.5 47.4 %copy-start.8 = (bf16[128,448]{0,1:T(8,128)(2,1)S(1)}, bf16[128,448]{0,1:T(8,128)(2,1)}, u32[]{:S(2)}) copy-start(bf16[128,448]{0,1:T(8,128)(2,1)} %param.11) | copy-start | bytes 344068
  84.1 44.4 %copy-start.9 = (bf16[128,448]{0,1:T(8,128)(2,1)S(1)}, bf16[128,448]{0,1:T(8,128)(2,1)}, u32[]{:S(2)}) copy-start(bf16[128,448]{0,1:T(8,128)(2,1)} %param.12) | copy-start | bytes 344068
  85.1 86.9 %all-to-all-start.2 = ((bf16[8,128,448]{1,2,0:T(8,128)(2,1)}), bf16[8,128,448]{1,2,0:T(8,128)(2,1)S(1)}, u32[]{:S(2)}, u32[]{:S(2)}) async-start(bf16[8,128,448]{1,2,0:T(8,128)(2,1)} %stack.2), calls=%async_computation.2 | async-start | bytes 1835008 | tf_op jit(solution)/shard_map/all_to_all | solution.py:35
  167.8 0.8 copy-start.4
  168.6 3.5 copy-start.1
  174.6 15.1 %copy-start.2 = (bf16[512,448]{0,1:T(8,128)(2,1)S(1)}, bf16[512,448]{0,1:T(8,128)(2,1)}, u32[]{:S(2)}) copy-start(bf16[512,448]{0,1:T(8,128)(2,1)} %all_gather.22) | copy-start | bytes 1376260
  174.6 15.1 %copy-start.3 = (bf16[512,448]{0,1:T(8,128)(2,1)S(1)}, bf16[512,448]{0,1:T(8,128)(2,1)}, u32[]{:S(2)}) copy-start(bf16[512,448]{0,1:T(8,128)(2,1)} %all_gather.21) | copy-start | bytes 1376260
  175.7 29.8 %all-to-all-start.3 = ((bf16[16,4,8,1024]{3,2,1,0:T(8,128)(2,1)}), bf16[16,4,8,1024]{3,2,1,0:T(8,128)(2,1)S(1)}, u32[]{:S(2)}, u32[]{:S(2)}) async-start(bf16[16,4,8,1024]{3,2,1,0:T(8,128)(2,1)} %bitcast.42), calls=%async_computation.3 | async-start | bytes 2097152 | tf_op jit(solution)/shard_map/all_to_all | solution.py:23
  190.5 19.2 %copy-start = (bf16[8,4096]{1,0:T(8,128)(2,1)S(1)}, bf16[8,4096]{1,0:T(8,128)(2,1)}, u32[]{:S(2)}) copy-start(bf16[8,4096]{1,0:T(8,128)(2,1)} %param.8) | copy-start | bytes 196612
  205.5 30.5 %all-to-all-start.5 = ((bf16[8,448,128]{2,1,0:T(8,128)(2,1)}), bf16[8,448,128]{2,1,0:T(8,128)(2,1)S(1)}, u32[]{:S(2)}, u32[]{:S(2)}) async-start(bf16[8,448,128]{2,1,0:T(8,128)(2,1)} %bitcast.44), calls=%async_computation.5 | async-start | bytes 1835008 | tf_op jit(solution)/shard_map/all_to_all | solution.py:23
  209.6 37.6 %copy-start.10 = (f32[4096]{0:T(1024)S(1)}, f32[4096]{0:T(1024)}, u32[]{:S(2)}) copy-start(f32[4096]{0:T(1024)} %param.15) | copy-start | bytes 49156
  209.6 132.9 %copy-start.5 = (bf16[8,4096]{1,0:T(8,128)(2,1)S(1)}, bf16[8,4096]{1,0:T(8,128)(2,1)}, u32[]{:S(2)}) copy-start(bf16[8,4096]{1,0:T(8,128)(2,1)} %param.9) | copy-start | bytes 196612
  236.0 11.0 %all-to-all-start.4 = ((f32[4,8,1024]{2,1,0:T(8,128)}), f32[4,8,1024]{2,1,0:T(8,128)S(1)}, u32[]{:S(2)}, u32[]{:S(2)}) async-start(f32[4,8,1024]{2,1,0:T(8,128)} %convert_reduce_fusion), calls=%async_computation.4 | async-start | bytes 262144 | tf_op jit(solution)/shard_map/all_to_all | solution.py:23
Sparse Core Ops, SparseCore 0:
  23.2 39.1 all-gather.1
